TPU v7x, 32 devices: a whole 2x2x4 slice. The times are simulated.
32 devices in a mesh: section: 2 (over x), dp: 16 (over z, y, core).
Axes of the slice: x: 2, y: 2, z: 4, core: 2. Of those that a mesh axis runs over, the one named last changes fastest.
Arguments:
- teacher_hidden: bfloat16 [64, 8192], P('dp'), may hold values from -12 to 12
- student_hidden: bfloat16 [64, 3584], P('dp'), may hold values from -12 to 12
- teacher_gain: bfloat16 [8192], replicated, may hold values from 0.5 to 1.5
- student_gain: bfloat16 [3584], replicated, may hold values from 0.5 to 1.5
- teacher_head: bfloat16 [5120, 8192], P(('section', 'dp')), may hold values from -64 to 64
- student_head: bfloat16 [5120, 3584], P(('section', 'dp')), may hold values from -64 to 64
- labels: int32 [64], replicated, may hold values from 0 to 5119
- cotangent: float32 [64], replicated, may hold values from 2 to 20
Outputs:
- loss: float32 [], replicated
- student_grad: float32 [64, 3584], P('dp')
- gain_grad: float32 [3584], replicated
- head_grad: bfloat16 [5120, 3584], P(('section', 'dp'))
All inputs are finite; a program needn't handle non-finite values.
Results may differ from a plain program's by a relative error of at most 0.0079.
Values may be sent and summed in bfloat16 or wider, within the bound.
A program may use at most 64 MiB of HBM per device.

v0:
```python
import jax
import jax.numpy as jnp
from jax import lax
from jax.sharding import PartitionSpec as P

eps = 1e-06
ce_weight = 0.5


def combined_all(part, axis, combine):
    gathered = jax.tree.map(lambda a: lax.all_gather(a, axis), part)

    def take(source):
        return jax.tree.map(lambda a: lax.dynamic_index_in_dim(a, source, 0, False), gathered)

    return lax.fori_loop(
        1, lax.axis_size(axis), lambda source, state: combine(state, take(source)), take(0)
    )


def normalize(hidden, gain):
    values = hidden.astype(jnp.float32)
    inverse = lax.rsqrt(jnp.mean(values * values, axis=-1, keepdims=True) + eps)
    scaled = values * inverse
    return (scaled, inverse, (scaled * gain.astype(jnp.float32)).astype(jnp.bfloat16))


def local_stats(teacher_logits, student_logits, picked_part):
    teacher_peak = jnp.max(teacher_logits, axis=1)
    student_peak = jnp.max(student_logits, axis=1)
    teacher_exp = jnp.exp(teacher_logits - teacher_peak[:, None])
    teacher_total = jnp.sum(teacher_exp, axis=1)
    cross = jnp.sum(teacher_exp * (teacher_logits - student_logits), axis=1)
    student_total = jnp.sum(jnp.exp(student_logits - student_peak[:, None]), axis=1)
    return (teacher_peak, teacher_total, cross, student_peak, student_total, picked_part)


def merge_stats(earlier, later):
    teacher_peak = jnp.maximum(earlier[0], later[0])
    first_scale = jnp.exp(earlier[0] - teacher_peak)
    second_scale = jnp.exp(later[0] - teacher_peak)
    student_peak = jnp.maximum(earlier[3], later[3])
    student_total = earlier[4] * jnp.exp(earlier[3] - student_peak) + later[4] * jnp.exp(
        later[3] - student_peak
    )
    return (
        teacher_peak,
        earlier[1] * first_scale + later[1] * second_scale,
        earlier[2] * first_scale + later[2] * second_scale,
        student_peak,
        student_total,
        earlier[5] + later[5],
    )


def on_device(
    teacher_hidden,
    student_hidden,
    teacher_gain,
    student_gain,
    teacher_head,
    student_head,
    labels,
    cotangent,
):
    _, _, teacher_normed = normalize(teacher_hidden, teacher_gain)
    scaled, inverse, student_normed = normalize(student_hidden, student_gain)
    teacher_rows, student_rows = (
        lax.all_gather(teacher_normed, "dp", axis=0, tiled=True),
        lax.all_gather(student_normed, "dp", axis=0, tiled=True),
    )
    teacher_logits = lax.dot_general(
        teacher_rows, teacher_head, (((1,), (1,)), ((), ())), preferred_element_type=jnp.float32
    )
    student_logits = lax.dot_general(
        student_rows, student_head, (((1,), (1,)), ((), ())), preferred_element_type=jnp.float32
    )
    entries = student_head.shape[0]
    offset = lax.axis_index(("section", "dp")) * entries
    columns = lax.broadcasted_iota(jnp.int32, student_logits.shape, 1) + offset
    hits = columns == labels[:, None]
    picked_part = jnp.sum(jnp.where(hits, student_logits, 0.0), axis=1)
    stats = combined_all(
        local_stats(teacher_logits, student_logits, picked_part), ("section", "dp"), merge_stats
    )
    teacher_peak, teacher_total, cross, student_peak, student_total, picked = stats
    teacher_log = teacher_peak + jnp.log(teacher_total)
    student_log = student_peak + jnp.log(student_total)
    token_loss = (
        cross / teacher_total - teacher_log + student_log + ce_weight * (student_log - picked)
    )
    loss = jnp.mean(token_loss)
    student_prob = jnp.exp(student_logits - student_log[:, None])
    teacher_prob = jnp.exp(teacher_logits - teacher_log[:, None])
    onehot = jnp.where(hits, 1.0, 0.0).astype(jnp.float32)
    slope = (
        cotangent[:, None] * ((1.0 + ce_weight) * student_prob - teacher_prob - ce_weight * onehot)
    ).astype(jnp.bfloat16)
    head_grad = lax.dot_general(
        slope, student_rows, (((0,), (0,)), ((), ())), preferred_element_type=jnp.float32
    ).astype(jnp.bfloat16)
    grad_terms = jnp.dot(slope, student_head, preferred_element_type=jnp.float32)
    gain_values = student_gain.astype(jnp.float32)
    row_part = lax.psum_scatter(grad_terms, "dp", scatter_dimension=0, tiled=True)
    normed_grad = lax.psum(row_part, "section")
    weighted = normed_grad * gain_values
    student_grad = inverse * (
        weighted - scaled * jnp.mean(weighted * scaled, axis=1, keepdims=True)
    )
    gain_grad = lax.psum(jnp.sum(normed_grad * scaled, axis=0), "dp")
    return (loss, student_grad, gain_grad, head_grad)


def solution(mesh):
    return jax.shard_map(
        on_device,
        mesh=mesh,
        in_specs=(
            P("dp", None),
            P("dp", None),
            P(),
            P(),
            P(("section", "dp"), None),
            P(("section", "dp"), None),
            P(),
            P(),
        ),
        out_specs=(P(), P("dp", None), P(), P(("section", "dp"), None)),
        check_vma=False,
    )
```

profile of v0, /device:TPU:0, one launch (start us, length us, event | category | flops | bytes accessed | tf_op | source)
XLA Modules:
  0.0 273.0 jit_solution(11768190820090649569)
XLA Ops:
  7.2 0.9 convert_element_type.26
  8.1 1.0 fusion.15
  9.1 1.6 fusion.27
  10.8 0.7 convert_element_type.29
  11.5 0.9 fusion.34
  12.4 0.8 fusion.35
  13.2 24.5 %all-gather.7 = bf16[16,4,3584]{2,1,0:T(4,128)(2,1)S(1)} all-gather(bf16[1,4,3584]{2,1,0:T(4,128)(2,1)S(1)} %fusion.35), channel_id=1, replica_groups=mesh['section'=2,'dp'=16] {'dp'}, dimensions={0}, use_global_device_ids=true | all-gather | bytes 487424 | tf_op jit(solution)/shard_map/all_gather | solution.py:70
  37.8 1.9 fusion.42
  40.0 11.6 %all-gather.10.cloned.1.call-done = bf16[16,4,8192]{2,1,0:T(4,128)(2,1)} async-done(((bf16[1,4,8192]{2,1,0:T(4,128)(2,1)}), bf16[16,4,8192]{2,1,0:T(4,128)(2,1)}) %all-gather.10.cloned.1.call-update) | async-done | bytes 1048592 | tf_op jit(solution)/shard_map/all_gather | solution.py:69
  51.6 2.1 reshape.67
  53.7 2.3 fusion.41
  56.1 0.3 dynamic-update-slice
  56.6 0.3 dynamic-update-slice.1
  57.6 39.2 %all-reduce.7 = (f32[2048]{0:T(1024)S(1)}, f32[2048]{0:T(1024)S(1)}, f32[2048]{0:T(1024)S(1)}, f32[2048]{0:T(1024)S(1)}, f32[2048]{0:T(1024)S(1)}, /*index=5*/f32[2048]{0:T(1024)S(1)}) all-reduce(f32[2048]{0:T(1024)S(1)} %dynamic-update-slice, f32[2048]{0:T(1024)S(1)} %dynamic-update-slice.1, ...), channel_id=2, replica_groups=mesh['section'=2,'dp'=16] {'section','dp'}, use_global_device_ids=true, to_apply=%add | all-reduce | flops 12288 | bytes 98304
  97.3 3.4 %while.25 = (s32[]{:T(128)}, f32[64]{0:T(128)S(1)}, f32[64]{0:T(128)S(1)}, f32[64]{0:T(128)S(1)}, f32[64]{0:T(128)S(1)}, /*index=5*/f32[64]{0:T(128)S(1)}, f32[6...) while((s32[]{:T(128)}, f32[64]{0:T(128)S(1)}, ...), condition=%wide.region_9.10_spmd, body=%wide.region_8.9_spmd.sunk | while | flops 1157 | bytes 6091 | solution.py:16
  100.7 0.6 add_reduce_fusion
  101.3 2.6 fusion.37
  104.0 0.6 dynamic-slice
  105.9 1.6 convolution_convert_fusion
  107.5 89.3 %all-reduce.10.cloned.1.call-done = f32[64,3584]{1,0:T(8,128)} async-done(((f32[64,3584]{1,0:T(8,128)}), f32[64,3584]{1,0:T(8,128)}) %all-reduce.10.cloned.1.call-update) | async-done | bytes 917520
  196.8 0.9 constant_dynamic-slice_fusion.6
  197.7 8.7 %psum.14 = f32[4,3584]{1,0:T(4,128)S(1)} all-reduce(f32[4,3584]{1,0:T(4,128)S(1)} %constant_dynamic-slice_fusion.6), channel_id=1, replica_groups=mesh['section'=2,'dp'=16] {'section'}, use_global_device_ids=true, to_apply=%region_12.13 | all-reduce | flops 14336 | bytes 114688 | tf_op jit(solution)/shard_map/psum | solution.py:105
  206.7 0.7 fusion.32
  207.4 57.6 %psum.15 = f32[3584]{0:T(1024)} all-reduce(f32[3584]{0:T(1024)S(1)} %get-tuple-element.323), channel_id=1, replica_groups=mesh['section'=2,'dp'=16] {'dp'}, use_global_device_ids=true, to_apply=%region_15.16 | all-reduce | flops 3584 | bytes 28672 | tf_op jit(solution)/shard_map/psum | solution.py:110
  (171 shorter events, 4.6 us)
Async XLA Ops:
  7.2 46.5 %copy-start = (bf16[160,8192]{1,0:T(8,128)(2,1)S(1)}, bf16[160,8192]{1,0:T(8,128)(2,1)}, u32[]{:S(2)}) copy-start(bf16[160,8192]{1,0:T(8,128)(2,1)} %param.14) | copy-start | bytes 7864324
  7.2 44.4 %all-gather.10.cloned.1.call-start = ((), (), s32[]{:S(2)}) async-start(), calls=%async_computation | async-start | bytes 1114112 | tf_op jit(solution)/shard_map/all_gather | solution.py:69
  10.7 186.1 %all-reduce.10.cloned.1.call-start = ((), (), s32[]{:S(2)}) async-start(), calls=%async_computation.1 | async-start | bytes 1835008
  12.4 0.8 copy-start.3
  53.7 2.6 copy-start.2
  53.7 47.6 %copy-start.5 = (f32[64]{0:T(128)S(1)}, f32[64]{0:T(128)}, u32[]{:S(2)}) copy-start(f32[64]{0:T(128)} %param.17) | copy-start | bytes 772
  101.3 2.7 copy-start.6
  104.0 102.5 %copy-start.1 = (bf16[4,3584]{1,0:T(4,128)(2,1)S(1)}, bf16[4,3584]{1,0:T(4,128)(2,1)}, u32[]{:S(2)}) copy-start(bf16[4,3584]{1,0:T(4,128)(2,1)} %param.11) | copy-start | bytes 86020
  104.0 102.5 %copy-start.4 = (f32[4]{0:T(128)S(1)}, f32[4]{0:T(128)}, u32[]{:S(2)}) copy-start(f32[4]{0:T(128)} %copy-done.3) | copy-start | bytes 52
Sparse Core Ops, SparseCore 0:
  10.8 40.6 all-gather.9
  104.1 92.6 all-reduce.9
where the time goes:
time: 274 us; the launch traced here: 273 us
  blocking collectives  130 us (47%)
  waiting for transfers between devices  101 us (37%)
  between operations  16.7 us (6%)
  other arithmetic  10 us (4%)
  matrix products  8.39 us (3%)
  local copies, waits for them, and re-layouts  5.89 us (2%)
    unnamed x3, waiting for transfers between devices  89.4 us
    psum x1, blocking collectives, on_device(): gain_grad = lax.psum(jnp.sum(normed_grad * scaled, axis=0), 'dp')  57.6 us
    unnamed x1, blocking collectives  39.2 us
    all_gather x1, blocking collectives, on_device(): lax.all_gather(student_normed, 'dp', axis=0, tiled=True)  24.5 us
    all_gather x1, waiting for transfers between devices, on_device(): lax.all_gather(teacher_normed, 'dp', axis=0, tiled=True)  11.6 us
    psum x1, blocking collectives, on_device(): normed_grad = lax.psum(row_part, 'section')  8.7 us
  transfers between devices with their start and end apart: 2, of which 2 were waited for; matrix products, arithmetic and copies ran while one was open for 3% of the time, Pallas kernels for 0%

commit v1 on v0

v1 whole, which is shorter than its diff:
```python
import functools

import jax
import jax.numpy as jnp
from jax import lax
from jax.experimental import pallas as pl
from jax.experimental.pallas import tpu as pltpu
from jax.sharding import PartitionSpec as P

eps = 1e-06
ce_weight = 0.5
f32 = jnp.float32
bf16 = jnp.bfloat16


def copy_to(source, target, sent, landed, section, position):
    return pltpu.make_async_remote_copy(
        src_ref=source,
        dst_ref=target,
        send_sem=sent,
        recv_sem=landed,
        device_id=(section, position),
        device_id_type=pl.DeviceIdType.MESH,
    )


def kernel(
    sections, n,
    th, sh, tg, sg, thead_hbm, shead_hbm, labels, cot,
    loss_out, sgrad_out, gain_out, hgrad_out,
    thead, shead, gt, gs, nt, ns, nsb, scf, tf, hg,
    st1, st2, csend1, crecv1, csend2, cbuf, gacc, esend, ebuf, g1, g2,
    load_sem, out_sem, rt, rs, zt, zs, yt, ys, ct, cs,
    s1s, s1r, s2s, s2r, c1s, c1r, c2s, c2r, es, er, g1s, g1r, g2s, g2r,
):
    S = sections
    A = n // 4
    chips = n // 2
    T = 4 * n
    DS = sh.shape[1]
    Dh = DS // 2
    entries = thead.shape[0]
    s = lax.axis_index("section")
    d = lax.axis_index("dp")
    a, b, c = d // 4, (d // 2) % 2, d % 2
    q = d // 2
    partner = q * 2 + (1 - c)

    def at(a_, b_, c_):
        return (a_ * 2 + b_) * 2 + c_

    across = at(a, 1 - b, c)

    load_t = pltpu.make_async_copy(thead_hbm, thead, load_sem.at[0])
    load_s = pltpu.make_async_copy(shead_hbm, shead, load_sem.at[1])
    load_t.start()
    load_s.start()

    total = S * n
    me = s * n + d
    barrier = pltpu.get_barrier_semaphore()

    def greet(k, carry):
        other = (me + k) % total
        pl.semaphore_signal(
            barrier, inc=1, device_id=(other // n, other % n),
            device_id_type=pl.DeviceIdType.MESH,
        )
        return carry

    lax.fori_loop(1, total, greet, 0)
    pl.semaphore_wait(barrier, total - 1)

    def both(src_t, src_s, slot, sem_t, sem_s, k, position):
        return (
            copy_to(src_s, gs.at[slot], sem_s.at[k], rs.at[slot], s, position),
            copy_to(src_t, gt.at[slot], sem_t.at[k], rt.at[slot], s, position),
        )

    def start(pair):
        for one in pair:
            one.start()

    def landed(slot):
        copy_to(gs.at[slot], gs.at[slot], ys.at[0], rs.at[slot], s, partner).wait_recv()
        copy_to(gt.at[slot], gt.at[slot], yt.at[0], rt.at[slot], s, partner).wait_recv()

    def along(k, carry):
        start(both(th, sh, d, zt, zs, k, at((a + k) % A, b, c)))
        return carry

    lax.fori_loop(1, A, along, 0)
    start(both(th, sh, d, yt, ys, 0, across))
    start(both(th, sh, d, ct, cs, 0, partner))
    gt[d] = th[...]
    gs[d] = sh[...]

    t_gain = tg[...].astype(f32)
    s_gain = sg[...].astype(f32)

    def process(p):
        x = jnp.concatenate([gs[2 * p].astype(f32), gs[2 * p + 1].astype(f32)], axis=0)
        inv = lax.rsqrt(jnp.mean(x * x, axis=1, keepdims=True) + eps)
        scaled = x * inv
        scf[p] = scaled
        ns[p] = scaled * s_gain
        y = jnp.concatenate([gt[2 * p].astype(f32), gt[2 * p + 1].astype(f32)], axis=0)
        inv_t = lax.rsqrt(jnp.mean(y * y, axis=1, keepdims=True) + eps)
        nt[p] = y * inv_t * t_gain

    def near(k, carry):
        slot = at((a - k + A) % A, b, c)
        landed(slot)
        start(both(gt.at[slot], gs.at[slot], slot, yt, ys, k, across))
        start(both(gt.at[slot], gs.at[slot], slot, ct, cs, k, partner))
        before = at((a - k + 1 + A) % A, b, 1 - c)
        landed(before)
        process(before // 2)
        return carry

    lax.fori_loop(1, A, near, 0)

    def far(k, carry):
        slot = at((a - k + A) % A, 1 - b, c)
        landed(slot)
        start(both(gt.at[slot], gs.at[slot], slot, ct, cs, A + k, partner))
        first = jnp.where(k == 0, 1, 0)
        before = at((a - k + 1 + A) % A, jnp.where(first == 1, b, 1 - b), 1 - c)
        landed(before)
        process(before // 2)
        return carry

    lax.fori_loop(0, A, far, 0)
    last = at((a - A + 1 + A) % A, 1 - b, 1 - c)
    landed(last)
    process(last // 2)

    nsb[...] = ns[...].reshape(T, DS).astype(bf16)
    load_s.wait()
    contract = (((1,), (1,)), ((), ()))
    sl = lax.dot_general(shead[...], nsb[...], contract, preferred_element_type=f32)
    load_t.wait()
    tl = lax.dot_general(
        thead[...], nt[...].reshape(T, nt.shape[2]).astype(bf16), contract,
        preferred_element_type=f32,
    )
    rows = lax.broadcasted_iota(jnp.int32, sl.shape, 0) + me * entries
    hits = rows == labels[...]

    tp = jnp.max(tl, axis=0, keepdims=True)
    sp = jnp.max(sl, axis=0, keepdims=True)
    te = jnp.exp(tl - tp)
    own1 = (s * 2 + b) * 2 + c
    stats = (
        tp,
        jnp.sum(te, axis=0, keepdims=True),
        jnp.sum(te * (tl - sl), axis=0, keepdims=True),
        sp,
        jnp.sum(jnp.exp(sl - sp), axis=0, keepdims=True),
        jnp.sum(jnp.where(hits, sl, 0.0), axis=0, keepdims=True),
    )

    def put(ref, slot, values):
        padded = list(values) + [jnp.zeros((8 - len(values), T), f32)]
        ref[slot] = jnp.concatenate(padded, axis=0)

    def merged(ref, count):
        tps = [ref[g, 0:1, :] for g in range(count)]
        sps = [ref[g, 3:4, :] for g in range(count)]
        tp = functools.reduce(jnp.maximum, tps)
        sp = functools.reduce(jnp.maximum, sps)
        tt = cr = stt = pk = 0.0
        for g in range(count):
            w = jnp.exp(tps[g] - tp)
            tt = tt + ref[g, 1:2, :] * w
            cr = cr + ref[g, 2:3, :] * w
            stt = stt + ref[g, 4:5, :] * jnp.exp(sps[g] - sp)
            pk = pk + ref[g, 5:6, :]
        return tp, tt, cr, sp, stt, pk

    def send_all(count, own, ref, sent, got, where):
        def go(k, carry):
            other = (own + k) % count
            copy_to(ref.at[own], ref.at[own], sent.at[k], got.at[own], *where(other)).start()
            return carry

        lax.fori_loop(1, count, go, 0)

    def wait_all(count, own, ref, got):
        def go(k, carry):
            other = (own + k) % count
            copy_to(ref.at[other], ref.at[other], got.at[other], got.at[other], s, partner).wait_recv()
            return carry

        lax.fori_loop(1, count, go, 0)

    def where1(g):
        return g // 4, at(a, (g // 2) % 2, g % 2)

    def where2(g):
        return s, at(g, b, c)

    put(st1, own1, stats)
    send_all(4 * S, own1, st1, s1s, s1r, where1)
    wait_all(4 * S, own1, st1, s1r)
    put(st2, a, merged(st1, 4 * S))
    send_all(A, a, st2, s2s, s2r, where2)
    wait_all(A, a, st2, s2r)
    tp, tt, cr, sp, stt, pk = merged(st2, A)

    t_log = tp + jnp.log(tt)
    s_log = sp + jnp.log(stt)
    token_loss = cr / tt - t_log + s_log + ce_weight * (s_log - pk)
    loss_out[...] = jnp.sum(token_loss, axis=1, keepdims=True) / T
    slope = (
        cot[...]
        * (
            (1.0 + ce_weight) * jnp.exp(sl - s_log)
            - jnp.exp(tl - t_log)
            - ce_weight * jnp.where(hits, 1.0, 0.0)
        )
    ).astype(bf16)

    tf[...] = lax.dot_general(
        slope, shead[...], (((0,), (0,)), ((), ())), preferred_element_type=f32
    ).reshape(chips, 8, DS)
    mine = pl.ds(pl.multiple_of(c * Dh, 128), Dh)
    theirs = pl.ds(pl.multiple_of((1 - c) * Dh, 128), Dh)
    csend1[...] = tf[:, :, theirs].astype(bf16)
    swap = copy_to(csend1, crecv1, c1s, c1r, s, partner)
    swap.start()
    hg[...] = jnp.dot(slope, nsb[...], preferred_element_type=f32).astype(bf16)
    store_h = pltpu.make_async_copy(hg, hgrad_out, out_sem)
    store_h.start()
    swap.wait_recv()

    gacc[...] = jnp.zeros_like(gacc)

    def chip_sum(p):
        block = tf[p, :, mine] + crecv1[p].astype(f32)
        gacc[...] += block * scf[p, :, mine]
        return block

    def scatter(k, carry):
        p = (q + k) % chips
        csend2[p] = chip_sum(p).astype(bf16)
        copy_to(csend2.at[p], cbuf.at[q], c2s.at[k], c2r.at[q], s, p * 2 + c).start()
        return carry

    lax.fori_loop(1, chips, scatter, 0)
    acc = chip_sum(q)

    own_g1 = s * 2 + b
    own_g2 = a * 2 + c
    g1[own_g1] = jnp.sum(gacc[...], axis=0, keepdims=True)
    send_all(2 * S, own_g1, g1, g1s, g1r, lambda g: (g // 2, at(a, g % 2, c)))
    wait_all(2 * S, own_g1, g1, g1r)
    g2[own_g2] = functools.reduce(jnp.add, [g1[g] for g in range(2 * S)])
    send_all(2 * A, own_g2, g2, g2s, g2r, lambda g: (s, at(g // 2, b, g % 2)))

    tf[q, :, mine] = acc

    def gather_sum(k, carry):
        p = (q - k + chips) % chips
        copy_to(cbuf.at[p], cbuf.at[p], c2s.at[0], c2r.at[p], s, partner).wait_recv()
        tf[q, :, mine] += cbuf[p].astype(f32)
        return carry

    lax.fori_loop(1, chips, gather_sum, 0)
    acc = tf[q, :, mine]
    esend[0] = acc[0:4]
    esend[1] = acc[4:8]
    own_e = s * 2 + c
    ebuf[own_e] = esend[c]

    def finish(k, carry):
        other = (own_e + k) % (2 * S)
        copy_to(
            esend.at[other % 2], ebuf.at[own_e], es.at[k], er.at[own_e],
            other // 2, q * 2 + other % 2,
        ).start()
        return carry

    lax.fori_loop(1, 2 * S, finish, 0)
    wait_all(2 * A, own_g2, g2, g2r)
    for h in range(2):
        gain_out[:, h * Dh:(h + 1) * Dh] = functools.reduce(
            jnp.add, [g2[2 * g + h] for g in range(A)]
        )
    x = sh[...].astype(f32)
    inverse = lax.rsqrt(jnp.mean(x * x, axis=1, keepdims=True) + eps)
    wait_all(2 * S, own_e, ebuf, er)
    sums = jnp.zeros((4, 1), f32)
    for h in range(2):
        part = slice(h * Dh, (h + 1) * Dh)
        grad = functools.reduce(jnp.add, [ebuf[2 * g + h] for g in range(S)])
        weighted = grad * s_gain[:, part]
        sgrad_out[:, part] = weighted
        sums = sums + jnp.sum(weighted * (x[:, part] * inverse), axis=1, keepdims=True)
    sgrad_out[...] = inverse * (sgrad_out[...] - (x * inverse) * (sums / DS))

    def sent(ref, sem):
        copy_to(ref, ref, sem, sem, s, partner).wait_send()

    def drain(ref, sems, low, high):
        def go(k, carry):
            sent(ref, sems.at[k])
            return carry

        lax.fori_loop(low, high, go, 0)

    drain(th, zt, 1, A)
    drain(sh, zs, 1, A)
    drain(th, yt, 0, A)
    drain(sh, ys, 0, A)
    drain(th, ct, 0, 2 * A)
    drain(sh, cs, 0, 2 * A)
    drain(st1.at[0], s1s, 1, 4 * S)
    drain(st2.at[0], s2s, 1, A)
    sent(csend1, c1s)
    drain(cbuf.at[0], c2s, 1, chips)
    drain(g1.at[0], g1s, 1, 2 * S)
    drain(g2.at[0], g2s, 1, 2 * A)
    drain(esend.at[0], es, 1, 2 * S)
    store_h.wait()


def on_device(
    sections, n,
    teacher_hidden, student_hidden, teacher_gain, student_gain,
    teacher_head, student_head, labels, cotangent,
):
    S, A, chips = sections, n // 4, n // 2
    T = 4 * n
    rows, DT = teacher_head.shape
    DS = student_head.shape[1]
    Dh = DS // 2
    vmem = pl.BlockSpec(memory_space=pltpu.VMEM)
    anywhere = pl.BlockSpec(memory_space=pl.ANY)
    sem = pltpu.SemaphoreType.DMA
    loss, grad, gain, head = pl.pallas_call(
        functools.partial(kernel, sections, n),
        out_shape=(
            jax.ShapeDtypeStruct((1, 1), f32),
            jax.ShapeDtypeStruct((4, DS), f32),
            jax.ShapeDtypeStruct((1, DS), f32),
            jax.ShapeDtypeStruct((rows, DS), bf16),
        ),
        in_specs=[vmem] * 4 + [anywhere] * 2 + [vmem] * 2,
        out_specs=(vmem, vmem, vmem, anywhere),
        scratch_shapes=[
            pltpu.VMEM((rows, DT), bf16),
            pltpu.VMEM((rows, DS), bf16),
            pltpu.VMEM((n, 4, DT), bf16),
            pltpu.VMEM((n, 4, DS), bf16),
            pltpu.VMEM((chips, 8, DT), f32),
            pltpu.VMEM((chips, 8, DS), f32),
            pltpu.VMEM((T, DS), bf16),
            pltpu.VMEM((chips, 8, DS), f32),
            pltpu.VMEM((chips, 8, DS), f32),
            pltpu.VMEM((rows, DS), bf16),
            pltpu.VMEM((4 * S, 8, T), f32),
            pltpu.VMEM((A, 8, T), f32),
            pltpu.VMEM((chips, 8, Dh), bf16),
            pltpu.VMEM((chips, 8, Dh), bf16),
            pltpu.VMEM((chips, 8, Dh), bf16),
            pltpu.VMEM((chips, 8, Dh), bf16),
            pltpu.VMEM((8, Dh), f32),
            pltpu.VMEM((2, 4, Dh), f32),
            pltpu.VMEM((2 * S, 4, Dh), f32),
            pltpu.VMEM((2 * S, 1, Dh), f32),
            pltpu.VMEM((2 * A, 1, Dh), f32),
            sem((2,)), sem,
            sem((n,)), sem((n,)),
            sem((A,)), sem((A,)), sem((A,)), sem((A,)), sem((2 * A,)), sem((2 * A,)),
            sem((4 * S,)), sem((4 * S,)), sem((A,)), sem((A,)),
            sem, sem, sem((chips,)), sem((chips,)),
            sem((2 * S,)), sem((2 * S,)), sem((2 * S,)), sem((2 * S,)),
            sem((2 * A,)), sem((2 * A,)),
        ],
        compiler_params=pltpu.CompilerParams(
            collective_id=0, has_side_effects=True, vmem_limit_bytes=60 * 1024 * 1024
        ),
        name="distill",
    )(
        teacher_hidden, student_hidden,
        teacher_gain.reshape(1, DT), student_gain.reshape(1, DS),
        teacher_head, student_head,
        labels.reshape(1, T), cotangent.reshape(1, T),
    )
    return loss[0, 0], grad, gain[0], head


def solution(mesh):
    return jax.shard_map(
        functools.partial(on_device, mesh.shape["section"], mesh.shape["dp"]),
        mesh=mesh,
        in_specs=(
            P("dp", None),
            P("dp", None),
            P(),
            P(),
            P(("section", "dp"), None),
            P(("section", "dp"), None),
            P(),
            P(),
        ),
        out_specs=(P(), P("dp", None), P(), P(("section", "dp"), None)),
        check_vma=False,
    )
```

time: 274 us -> 55.3 us (0.20)
  blocking collectives: 130 us -> 0 us
  waiting for transfers between devices: 101 us -> 0 us
  Pallas kernels: 0 us -> 44.4 us
  between operations: 16.7 us -> 2.41 us
  other arithmetic: 10 us -> 1.36 us
  matrix products: 8.39 us -> 0 us
    unnamed x3 -> x0, waiting for transfers between devices: 89.4 us -> none
    psum x2 -> x0, blocking collectives: 66.3 us -> none  [the longest x1 57.6 us: on_device(): gain_grad = lax.psum(jnp.sum(normed_grad * scaled, axis=0), 'dp')]
    pallas_call x0 -> x1, Pallas kernels: none -> 44.4 us  [on_device(): pl.pallas_call(functools.partial(kernel, sections, n), out_shape=(jax.Sha...]
    unnamed x1 -> x0, blocking collectives: 39.2 us -> none
    all_gather x1 -> x0, blocking collectives: 24.5 us -> none  [on_device(): lax.all_gather(student_normed, 'dp', axis=0, tiled=True)]
    all_gather x1 -> x0, waiting for transfers between devices: 11.6 us -> none  [on_device(): lax.all_gather(teacher_normed, 'dp', axis=0, tiled=True)]
    dot_general x4 -> x0, matrix products: 8.39 us -> none  [the longest x1 2.61 us: on_device(): jnp.dot(slope, student_head, preferred_element_type=jnp.float32)]
    reduce_sum x5 -> x0, other arithmetic: 2.97 us -> none  [the longest x2 1.91 us: normalize(): inverse = lax.rsqrt(jnp.mean(values * values, axis=-1, keepdims=True) + eps)]
  transfers between devices with their start and end apart: 2 -> 0, of which waited for: 2 -> 0; matrix products, arithmetic and copies ran while one was open for 3% -> 0% of each run, Pallas kernels for 0% -> 0%
where the time goes in v1:
time: 55.3 us; the launch traced here: 54.6 us
  Pallas kernels  44.4 us (80%)
  local copies, waits for them, and re-layouts  6.43 us (12%)
  between operations  2.41 us (4%)
  other arithmetic  1.36 us (2%)
    pallas_call x1, Pallas kernels, on_device(): pl.pallas_call(functools.partial(kernel, sections, n), out_shape=(jax.Sha...  44.4 us
    unnamed x2, local copies, waits for them, and re-layouts  3.78 us
    pallas_call x1, other arithmetic, on_device(): pl.pallas_call(functools.partial(kernel, sections, n), out_shape=(jax.Sha...  1.36 us
    reshape x1, local copies, waits for them, and re-layouts, on_device(): teacher_gain.reshape(1, DT)  1.35 us
    reshape x1, local copies, waits for them, and re-layouts, on_device(): student_gain.reshape(1, DS)  1.3 us

profile of v1, /device:TPU:0, one launch (start us, length us, event | category | flops | bytes accessed | tf_op | source)
XLA Modules:
  0.0 54.6 jit_solution(15913020413750984943)
XLA Ops:
  0.6 1.4 %reshape.20.tg = bf16[1,8192]{1,0:T(2,128)(2,1)} reshape(bf16[8192]{0:T(1024)(128)(2,1)} %param.10) | data formatting | bytes 32768 | tf_op jit(solution)/shard_map/reshape | solution.py:387
  2.0 1.3 %reshape.21.sg = bf16[1,3584]{1,0:T(2,128)(2,1)} reshape(bf16[3584]{0:T(1024)(128)(2,1)} %param.11) | data formatting | bytes 14336 | tf_op jit(solution)/shard_map/reshape | solution.py:387
  3.3 44.4 %distill.1 = (f32[1,1]{1,0:T(1,128)}, f32[4,3584]{1,0:T(4,128)}, f32[1,3584]{1,0:T(1,128)}, bf16[160,3584]{1,0:T(8,128)(2,1)}) custom-call(bf16[4,8192]{1,0:T(4,128)(2,1)} %th.1, bf16[4,3584]{1,0:T(4,128)(2,1)} %sh.1, bf16[1,8192]{1,0:T(2,128)(2,1)} %reshape.20.tg, bf16[1,3584]{1,0:T(2,128)(2,1)} %reshape.21.sg, bf16[160,8192]{1,0:T(8,128)(2,1)} %thead_hbm.1, ...), custom_call_target="tpu_custom_call" | custom-call | tf_op jit(solution)/shard_map/distill/pallas_call | solution.py:341
  47.7 1.4 %reduce = f32[3584]{0:T(1024)} reduce(f32[1,3584]{1,0:T(1,128)} %get-tuple-element.10, f32[]{:T(128)} %constant.2), dimensions={0}, to_apply=%get-tuple-element.10.reduce_sub_computation | reduce | bytes 28676 | tf_op jit(solution)/shard_map/distill/pallas_call | solution.py:341
  49.7 1.4 %copy.16 = f32[4,3584]{1,0:T(4,128)} copy(f32[4,3584]{1,0:T(4,128)} %get-tuple-element.17) | data formatting | bytes 114688
  51.2 2.3 %copy.17 = bf16[160,3584]{1,0:T(8,128)(2,1)} copy(bf16[160,3584]{1,0:T(8,128)(2,1)} %get-tuple-element.19) | data formatting | bytes 2293760

commit v2 on v1

--- a/solution.py
+++ b/solution.py
@@ -26,17 +26,18 @@
 
 def kernel(
     sections, n,
-    th, sh, tg, sg, thead_hbm, shead_hbm, labels, cot,
-    loss_out, sgrad_out, gain_out, hgrad_out,
-    thead, shead, gt, gs, nt, ns, nsb, scf, tf, hg,
+    th_hbm, sh_hbm, tg_hbm, sg_hbm, thead_hbm, shead_hbm, labels_hbm, cot_hbm,
+    loss_out, sgrad_out, gain_out, slope_out, nsb_out,
+    thead, shead, th, sh, tg, sg, labels, cot, tgr, sgr, gt, gs, nt, ns, nsb, scf, tf,
     st1, st2, csend1, crecv1, csend2, cbuf, gacc, esend, ebuf, g1, g2,
-    load_sem, out_sem, rt, rs, zt, zs, yt, ys, ct, cs,
+    load_sem, out_sem, in_sem, rt, rs, zt, zs, yt, ys, ct, cs,
     s1s, s1r, s2s, s2r, c1s, c1r, c2s, c2r, es, er, g1s, g1r, g2s, g2r,
 ):
     S = sections
     A = n // 4
     chips = n // 2
-    T = 4 * n
+    R = th.shape[0]
+    T = R * n
     DS = sh.shape[1]
     Dh = DS // 2
     entries = thead.shape[0]
@@ -51,10 +52,14 @@
 
     across = at(a, 1 - b, c)
 
+    small = [
+        pltpu.make_async_copy(source, target, in_sem.at[i])
+        for i, (source, target) in enumerate(
+            ((th_hbm, th), (sh_hbm, sh), (tg_hbm, tg), (sg_hbm, sg), (labels_hbm, labels), (cot_hbm, cot))
+        )
+    ]
     load_t = pltpu.make_async_copy(thead_hbm, thead, load_sem.at[0])
     load_s = pltpu.make_async_copy(shead_hbm, shead, load_sem.at[1])
-    load_t.start()
-    load_s.start()
 
     total = S * n
     me = s * n + d
@@ -69,6 +74,12 @@
         return carry
 
     lax.fori_loop(1, total, greet, 0)
+    for one in small:
+        one.start()
+    load_s.start()
+    load_t.start()
+    for one in small:
+        one.wait()
     pl.semaphore_wait(barrier, total - 1)
 
     def both(src_t, src_s, slot, sem_t, sem_s, k, position):
@@ -95,18 +106,21 @@
     gt[d] = th[...]
     gs[d] = sh[...]
 
-    t_gain = tg[...].astype(f32)
-    s_gain = sg[...].astype(f32)
+    for source, target in ((tg, tgr), (sg, sgr)):
+        values = source[...].astype(f32)
+        for i in range(source.shape[0]):
+            target[:, i * 128:(i + 1) * 128] = values[i:i + 1, :]
+    s_gain = sgr[...]
 
     def process(p):
         x = jnp.concatenate([gs[2 * p].astype(f32), gs[2 * p + 1].astype(f32)], axis=0)
         inv = lax.rsqrt(jnp.mean(x * x, axis=1, keepdims=True) + eps)
         scaled = x * inv
         scf[p] = scaled
-        ns[p] = scaled * s_gain
+        ns[p] = scaled * sgr[...]
         y = jnp.concatenate([gt[2 * p].astype(f32), gt[2 * p + 1].astype(f32)], axis=0)
         inv_t = lax.rsqrt(jnp.mean(y * y, axis=1, keepdims=True) + eps)
-        nt[p] = y * inv_t * t_gain
+        nt[p] = y * inv_t * tgr[...]
 
     def near(k, carry):
         slot = at((a - k + A) % A, b, c)
@@ -223,15 +237,15 @@
 
     tf[...] = lax.dot_general(
         slope, shead[...], (((0,), (0,)), ((), ())), preferred_element_type=f32
-    ).reshape(chips, 8, DS)
+    ).reshape(chips, 2 * R, DS)
     mine = pl.ds(pl.multiple_of(c * Dh, 128), Dh)
     theirs = pl.ds(pl.multiple_of((1 - c) * Dh, 128), Dh)
     csend1[...] = tf[:, :, theirs].astype(bf16)
     swap = copy_to(csend1, crecv1, c1s, c1r, s, partner)
     swap.start()
-    hg[...] = jnp.dot(slope, nsb[...], preferred_element_type=f32).astype(bf16)
-    store_h = pltpu.make_async_copy(hg, hgrad_out, out_sem)
-    store_h.start()
+    slope_out[...] = slope
+    store_n = pltpu.make_async_copy(nsb, nsb_out, out_sem)
+    store_n.start()
     swap.wait_recv()
 
     gacc[...] = jnp.zeros_like(gacc)
@@ -268,8 +282,8 @@
 
     lax.fori_loop(1, chips, gather_sum, 0)
     acc = tf[q, :, mine]
-    esend[0] = acc[0:4]
-    esend[1] = acc[4:8]
+    esend[0] = acc[0:R]
+    esend[1] = acc[R:2 * R]
     own_e = s * 2 + c
     ebuf[own_e] = esend[c]
 
@@ -290,7 +304,7 @@
     x = sh[...].astype(f32)
     inverse = lax.rsqrt(jnp.mean(x * x, axis=1, keepdims=True) + eps)
     wait_all(2 * S, own_e, ebuf, er)
-    sums = jnp.zeros((4, 1), f32)
+    sums = jnp.zeros((R, 1), f32)
     for h in range(2):
         part = slice(h * Dh, (h + 1) * Dh)
         grad = functools.reduce(jnp.add, [ebuf[2 * g + h] for g in range(S)])
@@ -322,7 +336,15 @@
     drain(g1.at[0], g1s, 1, 2 * S)
     drain(g2.at[0], g2s, 1, 2 * A)
     drain(esend.at[0], es, 1, 2 * S)
-    store_h.wait()
+    store_n.wait()
+
+
+def finish_kernel(slope, normed, loss, grad, gain, loss_out, grad_out, gain_out, head_out):
+    head_out[...] = jnp.dot(slope[...], normed[...], preferred_element_type=f32).astype(bf16)
+    loss_out[...] = loss[...]
+    grad_out[...] = grad[...]
+    for i in range(gain_out.shape[0]):
+        gain_out[i:i + 1, :] = gain[:, i * 128:(i + 1) * 128]
 
 
 def on_device(
@@ -331,46 +353,55 @@
     teacher_head, student_head, labels, cotangent,
 ):
     S, A, chips = sections, n // 4, n // 2
-    T = 4 * n
+    R = teacher_hidden.shape[0]
+    T = R * n
     rows, DT = teacher_head.shape
     DS = student_head.shape[1]
     Dh = DS // 2
     vmem = pl.BlockSpec(memory_space=pltpu.VMEM)
     anywhere = pl.BlockSpec(memory_space=pl.ANY)
     sem = pltpu.SemaphoreType.DMA
-    loss, grad, gain, head = pl.pallas_call(
+    loss, grad, gain, slope, normed = pl.pallas_call(
         functools.partial(kernel, sections, n),
         out_shape=(
             jax.ShapeDtypeStruct((1, 1), f32),
-            jax.ShapeDtypeStruct((4, DS), f32),
+            jax.ShapeDtypeStruct((R, DS), f32),
             jax.ShapeDtypeStruct((1, DS), f32),
-            jax.ShapeDtypeStruct((rows, DS), bf16),
+            jax.ShapeDtypeStruct((rows, T), bf16),
+            jax.ShapeDtypeStruct((T, DS), bf16),
         ),
-        in_specs=[vmem] * 4 + [anywhere] * 2 + [vmem] * 2,
-        out_specs=(vmem, vmem, vmem, anywhere),
+        in_specs=[anywhere] * 8,
+        out_specs=(vmem, vmem, vmem, vmem, anywhere),
         scratch_shapes=[
             pltpu.VMEM((rows, DT), bf16),
             pltpu.VMEM((rows, DS), bf16),
-            pltpu.VMEM((n, 4, DT), bf16),
-            pltpu.VMEM((n, 4, DS), bf16),
-            pltpu.VMEM((chips, 8, DT), f32),
-            pltpu.VMEM((chips, 8, DS), f32),
+            pltpu.VMEM((R, DT), bf16),
+            pltpu.VMEM((R, DS), bf16),
+            pltpu.VMEM((DT // 128, 128), bf16),
+            pltpu.VMEM((DS // 128, 128), bf16),
+            pltpu.VMEM((1, T), jnp.int32),
+            pltpu.VMEM((1, T), f32),
+            pltpu.VMEM((1, DT), f32),
+            pltpu.VMEM((1, DS), f32),
+            pltpu.VMEM((n, R, DT), bf16),
+            pltpu.VMEM((n, R, DS), bf16),
+            pltpu.VMEM((chips, 2 * R, DT), f32),
+            pltpu.VMEM((chips, 2 * R, DS), f32),
             pltpu.VMEM((T, DS), bf16),
-            pltpu.VMEM((chips, 8, DS), f32),
-            pltpu.VMEM((chips, 8, DS), f32),
-            pltpu.VMEM((rows, DS), bf16),
+            pltpu.VMEM((chips, 2 * R, DS), f32),
+            pltpu.VMEM((chips, 2 * R, DS), f32),
             pltpu.VMEM((4 * S, 8, T), f32),
             pltpu.VMEM((A, 8, T), f32),
-            pltpu.VMEM((chips, 8, Dh), bf16),
-            pltpu.VMEM((chips, 8, Dh), bf16),
-            pltpu.VMEM((chips, 8, Dh), bf16),
-            pltpu.VMEM((chips, 8, Dh), bf16),
-            pltpu.VMEM((8, Dh), f32),
-            pltpu.VMEM((2, 4, Dh), f32),
-            pltpu.VMEM((2 * S, 4, Dh), f32),
+            pltpu.VMEM((chips, 2 * R, Dh), bf16),
+            pltpu.VMEM((chips, 2 * R, Dh), bf16),
+            pltpu.VMEM((chips, 2 * R, Dh), bf16),
+            pltpu.VMEM((chips, 2 * R, Dh), bf16),
+            pltpu.VMEM((2 * R, Dh), f32),
+            pltpu.VMEM((2, R, Dh), f32),
+            pltpu.VMEM((2 * S, R, Dh), f32),
             pltpu.VMEM((2 * S, 1, Dh), f32),
             pltpu.VMEM((2 * A, 1, Dh), f32),
-            sem((2,)), sem,
+            sem((2,)), sem, sem((6,)),
             sem((n,)), sem((n,)),
             sem((A,)), sem((A,)), sem((A,)), sem((A,)), sem((2 * A,)), sem((2 * A,)),
             sem((4 * S,)), sem((4 * S,)), sem((A,)), sem((A,)),
@@ -384,11 +415,36 @@
         name="distill",
     )(
         teacher_hidden, student_hidden,
-        teacher_gain.reshape(1, DT), student_gain.reshape(1, DS),
+        teacher_gain.reshape(DT // 128, 128), student_gain.reshape(DS // 128, 128),
         teacher_head, student_head,
         labels.reshape(1, T), cotangent.reshape(1, T),
     )
-    return loss[0, 0], grad, gain[0], head
+    steps = 4
+    width = DS // steps
+
+    def whole(*shape):
+        return pl.BlockSpec(shape, lambda i: (0, 0))
+
+    loss, grad, gain, head = pl.pallas_call(
+        finish_kernel,
+        grid=(steps,),
+        out_shape=(
+            jax.ShapeDtypeStruct((1, 1), f32),
+            jax.ShapeDtypeStruct((R, DS), f32),
+            jax.ShapeDtypeStruct((DS // 128, 128), f32),
+            jax.ShapeDtypeStruct((rows, DS), bf16),
+        ),
+        in_specs=[
+            whole(rows, T), pl.BlockSpec((T, width), lambda i: (0, i)),
+            whole(1, 1), whole(R, DS), whole(1, DS),
+        ],
+        out_specs=(
+            whole(1, 1), whole(R, DS), whole(DS // 128, 128),
+            pl.BlockSpec((rows, width), lambda i: (0, i)),
+        ),
+        name="head",
+    )(slope, normed, loss, grad, gain)
+    return loss[0, 0], grad, gain.reshape(DS), head
 
 
 def solution(mesh):

time: 55.3 us -> 48.5 us (0.88)
  local copies, waits for them, and re-layouts: 6.43 us -> 0 us
  Pallas kernels: 44.4 us -> 47.6 us
  between operations: 2.41 us -> 0.64 us
  other arithmetic: 1.36 us -> 0 us
    pallas_call x0 -> x1, Pallas kernels: none -> 4.36 us  [on_device(): pl.pallas_call(finish_kernel, grid=(steps,), out_shape=(jax.ShapeDtypeStr...]
    unnamed x2 -> x0, local copies, waits for them, and re-layouts: 3.78 us -> none
    reshape x2 -> x0, local copies, waits for them, and re-layouts: 2.66 us -> none  [the longest x1 1.35 us: on_device(): teacher_gain.reshape(1, DT)]
    pallas_call x1 -> x0, other arithmetic: 1.36 us -> none  [on_device(): pl.pallas_call(functools.partial(kernel, sections, n), out_shape=(jax.Sha...]
    pallas_call x1, Pallas kernels: 44.4 us -> 43.3 us  [on_device(): pl.pallas_call(functools.partial(kernel, sections, n), out_shape=(jax.Sha...]
where the time goes in v2:
time: 48.5 us; the launch traced here: 48.3 us
  Pallas kernels  47.6 us (98%)
  between operations  0.64 us (1%)
    pallas_call x1, Pallas kernels, on_device(): pl.pallas_call(functools.partial(kernel, sections, n), out_shape=(jax.Sha...  43.3 us
    pallas_call x1, Pallas kernels, on_device(): pl.pallas_call(finish_kernel, grid=(steps,), out_shape=(jax.ShapeDtypeStr...  4.36 us

profile of v2, /device:TPU:0, one launch (start us, length us, event | category | flops | bytes accessed | tf_op | source)
XLA Modules:
  0.0 48.3 jit_solution(6898919934001941307)
XLA Ops:
  0.6 43.3 %distill.1 = (f32[1,1]{1,0:T(1,128)}, f32[4,3584]{1,0:T(4,128)}, f32[1,3584]{1,0:T(1,128)}, bf16[160,64]{1,0:T(8,128)(2,1)}, bf16[64,3584]{1,0:T(8,128)(2,1)}) custom-call(bf16[4,8192]{1,0:T(4,128)(2,1)} %th_hbm.1, bf16[4,3584]{1,0:T(4,128)(2,1)} %sh_hbm.1, bf16[64,128]{1,0:T(8,128)(2,1)} %bitcast.6, bf16[28,128]{1,0:T(8,128)(2,1)} %bitcast.7, ...), custom_call_target="tpu_custom_call" | custom-call | tf_op jit(solution)/shard_map/distill/pallas_call | solution.py:364
  43.9 4.4 %head.1 = (f32[1,1]{1,0:T(1,128)}, f32[4,3584]{1,0:T(4,128)}, f32[28,128]{1,0:T(8,128)}, bf16[160,3584]{1,0:T(8,128)(2,1)}) custom-call(bf16[160,64]{1,0:T(8,128)(2,1)} %get-tuple-element.13.slope, bf16[64,3584]{1,0:T(8,128)(2,1)} %get-tuple-element.14.normed, f32[1,1]{1,0:T(1,128)} %get-tuple-element.15.loss, f32[4,3584]{1,0:T(4,128)} %get-tuple-element.16.grad, ...), custom_call_target="tpu_custom_call" | custom-call | tf_op jit(solution)/shard_map/head/pallas_call | solution.py:428
